TPU v7x, 32 devices: a whole 2x2x4 slice. The times are simulated.
32 devices in a mesh: samp: 16 (over z, y, x), tp: 2 (over core).
Axes of the slice: x: 2, y: 2, z: 4, core: 2. Of those that a mesh axis runs over, the one named last changes fastest.
Arguments:
- images: bfloat16 [128, 12288], P(None, 'tp'), may hold values from -6 to 6
- enc_mean: float32 [128, 128], replicated, may hold values from -0.3 to 0.3
- enc_logscale: float32 [128, 128], replicated, may hold values from -0.15 to 0
- noise: float32 [128, 128, 128], P(None, 'samp'), may hold values from -5 to 5
- w_in: bfloat16 [128, 1024], P(None, 'tp'), may hold values from -0.5 to 0.5
- b_in: bfloat16 [1, 1024], P(None, 'tp'), may hold values from -3 to 3
- w_out: bfloat16 [1024, 12288], P(None, 'tp'), may hold values from -0.0078125 to 0.0078125
- b_out: float32 [1, 12288], P(None, 'tp'), may hold values from -3 to 3
- pixel_logscale: float32 [1, 12288], P(None, 'tp'), may hold values from 0 to 1
Outputs:
- bound: float32 [128], replicated
- log_weights: float32 [128, 128], P(None, 'samp')
All inputs are finite; a program needn't handle non-finite values.
Results may differ from a plain program's by a relative error of at most 0.00073.
Values may be sent and summed in bfloat16 or wider, within the bound.
No kernel may reach another device: no remote copies, remote signals or barrier semaphores. Data moves between devices by JAX's collectives and lax.ppermute only.
A program may use at most 64 MiB of HBM per device.

v0:
```python
import math

import jax
import jax.numpy as jnp
from jax import lax
from jax.sharding import PartitionSpec as P

HALF_LOG_TAU = 0.9189385332046727


def on_device(images, enc_mean, enc_logscale, noise, w_in, b_in, w_out, b_out, pixel_logscale):
    image_count, sample_count, latent_dims = noise.shape
    latent = enc_mean[:, None, :] + jnp.exp(enc_logscale)[:, None, :] * noise
    latent_rows = latent.reshape(image_count * sample_count, latent_dims).astype(jnp.bfloat16)
    w_whole, b_whole = (
        lax.all_gather(w_in, "tp", axis=1, tiled=True),
        lax.all_gather(b_in, "tp", axis=1, tiled=True),
    )
    hidden = jax.nn.relu(
        jnp.dot(latent_rows, w_whole, preferred_element_type=jnp.float32)
        + b_whole.astype(jnp.float32)
    ).astype(jnp.bfloat16)
    pixel_share = images.shape[1]
    all_pixels = pixel_share * lax.axis_size("tp")
    piece_width = math.gcd(pixel_share, 1024)
    piece_count = pixel_share // piece_width
    inverse = jnp.exp(-pixel_logscale)
    share_constant = -jnp.sum(pixel_logscale) - pixel_share * HALF_LOG_TAU

    def add_piece(position, running):
        offset = position * piece_width
        w_piece = lax.dynamic_slice_in_dim(w_out, offset, piece_width, 1)
        bias_piece = lax.dynamic_slice_in_dim(b_out, offset, piece_width, 1)
        inverse_piece = lax.dynamic_slice_in_dim(inverse, offset, piece_width, 1)
        image_piece = lax.dynamic_slice_in_dim(images, offset, piece_width, 1)
        pixel_mean = jnp.dot(hidden, w_piece, preferred_element_type=jnp.float32) + bias_piece
        pixel_mean = pixel_mean.reshape(image_count, sample_count, piece_width)
        scaled = (image_piece[:, None, :].astype(jnp.float32) - pixel_mean) * inverse_piece[
            None, :, :
        ]
        return running + jnp.sum(-0.5 * scaled * scaled, axis=2)

    partial_loglik = (
        lax.fori_loop(
            0, piece_count, add_piece, jnp.zeros((image_count, sample_count), jnp.float32)
        )
        + share_constant
    )
    prior = jnp.sum(-0.5 * latent * latent - HALF_LOG_TAU, axis=2)
    posterior = jnp.sum(-0.5 * noise * noise - enc_logscale[:, None, :] - HALF_LOG_TAU, axis=2)
    loglik = lax.psum(partial_loglik, "tp")
    logw = loglik + prior - posterior
    local_peak = jnp.max(logw, axis=1)
    peak = lax.pmax(local_peak, "samp")
    sum_exp = lax.psum(jnp.sum(jnp.exp(logw - peak[:, None]), axis=1), "samp")
    all_samples = sample_count * lax.axis_size("samp")
    bound = (peak + jnp.log(sum_exp) - jnp.log(jnp.float32(all_samples))) / all_pixels
    log_weights = (
        logw - peak[:, None] - jnp.log(sum_exp)[:, None] + jnp.log(jnp.float32(all_samples))
    )
    return (bound, log_weights)


def solution(mesh):
    in_specs = (
        P(None, "tp"),
        P(),
        P(),
        P(None, "samp", None),
        P(None, "tp"),
        P(None, "tp"),
        P(None, "tp"),
        P(None, "tp"),
        P(None, "tp"),
    )
    out_specs = (P(), P(None, "samp"))
    return jax.shard_map(
        on_device, mesh=mesh, in_specs=in_specs, out_specs=out_specs, check_vma=False
    )
```

profile of v0, /device:TPU:0, one launch (start us, length us, event | category | flops | bytes accessed | tf_op | source)
XLA Modules:
  0.0 188.4 jit_solution(797762416121667181)
XLA Ops:
  0.6 0.9 exp.9
  1.5 2.3 %all_gather.6 = bf16[128,1024]{1,0:T(8,128)(2,1)S(1)} all-gather(bf16[128,512]{1,0:T(8,128)(2,1)} %param.15), channel_id=1, replica_groups=mesh['samp'=16,'tp'=2] {'tp'}, dimensions={1}, use_global_device_ids=true | all-gather | bytes 393216 | tf_op jit(solution)/shard_map/all_gather | solution.py:16
  3.8 2.0 %all_gather.7 = bf16[1,1024]{1,0:T(2,128)(2,1)S(1)} all-gather(bf16[1,512]{1,0:T(2,128)(2,1)} %param.16), channel_id=1, replica_groups=mesh['samp'=16,'tp'=2] {'tp'}, dimensions={1}, use_global_device_ids=true | all-gather | bytes 3072 | tf_op jit(solution)/shard_map/all_gather | solution.py:17
  5.8 1.7 maximum_convert_fusion
  7.6 1.4 fusion.18
  9.0 93.3 %while.14 = (s32[]{:T(128)}, f32[128,8]{1,0:T(8,128)S(1)}, bf16[128,6144]{1,0:T(8,128)(2,1)}, bf16[1024,6144]{1,0:T(8,128)(2,1)}, bf16[1024,1024]{1,0:T(8,128)(2...) while((s32[]{:T(128)}, f32[128,8]{1,0:T(8,128)S(1)}, ...), condition=%wide.region_2.0_spmd.clone, body=%wide.region_0.0_spmd.clone.sunk | while | flops 2153907200 | bytes 22331568 | solution.py:44
  9.0 0.8 constant_dynamic-slice_fusion.3
  9.7 1.0 dynamic-slice_convert_fusion.2
  10.7 2.5 %broadcast_bitcast_fusion.2 = f32[1024,1024]{1,0:T(8,128)} fusion(f32[128,1024]{1,0:T(8,128)S(1)} %dynamic-slice_convert_fusion.2), kind=kLoop, calls=%fused_computation.6.clone.1 | loop fusion | bytes 4718592 | tf_op jit(solution)/shard_map/while/body/eval_jaxpr/sub | solution.py:38
  13.2 5.3 %copy.17 = f32[1024,1024]{0,1:T(8,128)} copy(f32[1024,1024]{1,0:T(8,128)} %broadcast_bitcast_fusion.2) | data formatting | bytes 8388608 | tf_op jit(solution)/shard_map/while/body/eval_jaxpr/sub | solution.py:38
  18.5 5.9 %fusion.27 = f32[1024]{0:T(1024)S(1)} fusion(f32[1024,1024]{0,1:T(8,128)} %copy.17, f32[1024]{0:T(1024)S(1)} %bitcast.26, f32[1024]{0:T(1024)S(1)} %bitcast.27, bf16[1024,1024]{1,0:T(8,128)(2,1)S(1)} %get-tuple-element.257, bf16[1024,6144]{1,0:T(8,128)(2,1)} %get-tuple-element.256, s32[]{:T(128)S(6)} %select_n.12), kind=kOutput, calls=%fused_computation.1.clone.1 | convolution fusion | flops 2153774080 | bytes 8400900 | tf_op jit(solution)/shard_map/while/body/eval_jaxpr/dot_general | solution.py:36
  24.6 0.7 constant_dynamic-slice_fusion.3
  25.3 1.0 dynamic-slice_convert_fusion.2
  26.3 2.5 %broadcast_bitcast_fusion.2 = f32[1024,1024]{1,0:T(8,128)} fusion(f32[128,1024]{1,0:T(8,128)S(1)} %dynamic-slice_convert_fusion.2), kind=kLoop, calls=%fused_computation.6.clone.1 | loop fusion | bytes 4718592 | tf_op jit(solution)/shard_map/while/body/eval_jaxpr/sub | solution.py:38
  28.7 5.3 %copy.17 = f32[1024,1024]{0,1:T(8,128)} copy(f32[1024,1024]{1,0:T(8,128)} %broadcast_bitcast_fusion.2) | data formatting | bytes 8388608 | tf_op jit(solution)/shard_map/while/body/eval_jaxpr/sub | solution.py:38
  34.0 5.9 %fusion.27 = f32[1024]{0:T(1024)S(1)} fusion(f32[1024,1024]{0,1:T(8,128)} %copy.17, f32[1024]{0:T(1024)S(1)} %bitcast.26, f32[1024]{0:T(1024)S(1)} %bitcast.27, bf16[1024,1024]{1,0:T(8,128)(2,1)S(1)} %get-tuple-element.257, bf16[1024,6144]{1,0:T(8,128)(2,1)} %get-tuple-element.256, s32[]{:T(128)S(6)} %select_n.12), kind=kOutput, calls=%fused_computation.1.clone.1 | convolution fusion | flops 2153774080 | bytes 8400900 | tf_op jit(solution)/shard_map/while/body/eval_jaxpr/dot_general | solution.py:36
  40.1 0.7 constant_dynamic-slice_fusion.3
  40.8 1.0 dynamic-slice_convert_fusion.2
  41.8 2.5 %broadcast_bitcast_fusion.2 = f32[1024,1024]{1,0:T(8,128)} fusion(f32[128,1024]{1,0:T(8,128)S(1)} %dynamic-slice_convert_fusion.2), kind=kLoop, calls=%fused_computation.6.clone.1 | loop fusion | bytes 4718592 | tf_op jit(solution)/shard_map/while/body/eval_jaxpr/sub | solution.py:38
  44.2 5.3 %copy.17 = f32[1024,1024]{0,1:T(8,128)} copy(f32[1024,1024]{1,0:T(8,128)} %broadcast_bitcast_fusion.2) | data formatting | bytes 8388608 | tf_op jit(solution)/shard_map/while/body/eval_jaxpr/sub | solution.py:38
  49.6 5.9 %fusion.27 = f32[1024]{0:T(1024)S(1)} fusion(f32[1024,1024]{0,1:T(8,128)} %copy.17, f32[1024]{0:T(1024)S(1)} %bitcast.26, f32[1024]{0:T(1024)S(1)} %bitcast.27, bf16[1024,1024]{1,0:T(8,128)(2,1)S(1)} %get-tuple-element.257, bf16[1024,6144]{1,0:T(8,128)(2,1)} %get-tuple-element.256, s32[]{:T(128)S(6)} %select_n.12), kind=kOutput, calls=%fused_computation.1.clone.1 | convolution fusion | flops 2153774080 | bytes 8400900 | tf_op jit(solution)/shard_map/while/body/eval_jaxpr/dot_general | solution.py:36
  55.5 0.1 reduce_sum.63
  55.6 0.7 constant_dynamic-slice_fusion.3
  56.3 1.0 dynamic-slice_convert_fusion.2
  57.3 2.5 %broadcast_bitcast_fusion.2 = f32[1024,1024]{1,0:T(8,128)} fusion(f32[128,1024]{1,0:T(8,128)S(1)} %dynamic-slice_convert_fusion.2), kind=kLoop, calls=%fused_computation.6.clone.1 | loop fusion | bytes 4718592 | tf_op jit(solution)/shard_map/while/body/eval_jaxpr/sub | solution.py:38
  59.8 5.3 %copy.17 = f32[1024,1024]{0,1:T(8,128)} copy(f32[1024,1024]{1,0:T(8,128)} %broadcast_bitcast_fusion.2) | data formatting | bytes 8388608 | tf_op jit(solution)/shard_map/while/body/eval_jaxpr/sub | solution.py:38
  65.1 5.9 %fusion.27 = f32[1024]{0:T(1024)S(1)} fusion(f32[1024,1024]{0,1:T(8,128)} %copy.17, f32[1024]{0:T(1024)S(1)} %bitcast.26, f32[1024]{0:T(1024)S(1)} %bitcast.27, bf16[1024,1024]{1,0:T(8,128)(2,1)S(1)} %get-tuple-element.257, bf16[1024,6144]{1,0:T(8,128)(2,1)} %get-tuple-element.256, s32[]{:T(128)S(6)} %select_n.12), kind=kOutput, calls=%fused_computation.1.clone.1 | convolution fusion | flops 2153774080 | bytes 8400900 | tf_op jit(solution)/shard_map/while/body/eval_jaxpr/dot_general | solution.py:36
  71.0 0.1 reduce_sum.63
  71.2 0.7 constant_dynamic-slice_fusion.3
  71.9 1.0 dynamic-slice_convert_fusion.2
  72.9 2.5 %broadcast_bitcast_fusion.2 = f32[1024,1024]{1,0:T(8,128)} fusion(f32[128,1024]{1,0:T(8,128)S(1)} %dynamic-slice_convert_fusion.2), kind=kLoop, calls=%fused_computation.6.clone.1 | loop fusion | bytes 4718592 | tf_op jit(solution)/shard_map/while/body/eval_jaxpr/sub | solution.py:38
  75.3 5.3 %copy.17 = f32[1024,1024]{0,1:T(8,128)} copy(f32[1024,1024]{1,0:T(8,128)} %broadcast_bitcast_fusion.2) | data formatting | bytes 8388608 | tf_op jit(solution)/shard_map/while/body/eval_jaxpr/sub | solution.py:38
  80.7 5.9 %fusion.27 = f32[1024]{0:T(1024)S(1)} fusion(f32[1024,1024]{0,1:T(8,128)} %copy.17, f32[1024]{0:T(1024)S(1)} %bitcast.26, f32[1024]{0:T(1024)S(1)} %bitcast.27, bf16[1024,1024]{1,0:T(8,128)(2,1)S(1)} %get-tuple-element.257, bf16[1024,6144]{1,0:T(8,128)(2,1)} %get-tuple-element.256, s32[]{:T(128)S(6)} %select_n.12), kind=kOutput, calls=%fused_computation.1.clone.1 | convolution fusion | flops 2153774080 | bytes 8400900 | tf_op jit(solution)/shard_map/while/body/eval_jaxpr/dot_general | solution.py:36
  86.6 0.1 reduce_sum.63
  86.7 0.7 constant_dynamic-slice_fusion.3
  87.4 1.0 dynamic-slice_convert_fusion.2
  88.4 2.5 %broadcast_bitcast_fusion.2 = f32[1024,1024]{1,0:T(8,128)} fusion(f32[128,1024]{1,0:T(8,128)S(1)} %dynamic-slice_convert_fusion.2), kind=kLoop, calls=%fused_computation.6.clone.1 | loop fusion | bytes 4718592 | tf_op jit(solution)/shard_map/while/body/eval_jaxpr/sub | solution.py:38
  90.8 5.3 %copy.17 = f32[1024,1024]{0,1:T(8,128)} copy(f32[1024,1024]{1,0:T(8,128)} %broadcast_bitcast_fusion.2) | data formatting | bytes 8388608 | tf_op jit(solution)/shard_map/while/body/eval_jaxpr/sub | solution.py:38
  96.2 5.9 %fusion.27 = f32[1024]{0:T(1024)S(1)} fusion(f32[1024,1024]{0,1:T(8,128)} %copy.17, f32[1024]{0:T(1024)S(1)} %bitcast.26, f32[1024]{0:T(1024)S(1)} %bitcast.27, bf16[1024,1024]{1,0:T(8,128)(2,1)S(1)} %get-tuple-element.257, bf16[1024,6144]{1,0:T(8,128)(2,1)} %get-tuple-element.256, s32[]{:T(128)S(6)} %select_n.12), kind=kOutput, calls=%fused_computation.1.clone.1 | convolution fusion | flops 2153774080 | bytes 8400900 | tf_op jit(solution)/shard_map/while/body/eval_jaxpr/dot_general | solution.py:36
  102.9 3.8 %psum.14 = f32[128,8]{1,0:T(8,128)S(1)} all-reduce(f32[128,8]{1,0:T(8,128)S(1)} %broadcast_add_fusion), channel_id=1, replica_groups=mesh['samp'=16,'tp'=2] {'tp'}, use_global_device_ids=true, to_apply=%region_4.5 | all-reduce | flops 1024 | bytes 8192 | tf_op jit(solution)/shard_map/psum | solution.py:51
  106.7 0.4 fusion.8
  107.1 0.1 fusion.17
  107.2 43.2 %pmax.7 = f32[128]{0:T(128)S(1)} all-reduce(f32[128]{0:T(128)S(1)} %get-tuple-element.176), channel_id=1, replica_groups=mesh['samp'=16,'tp'=2] {'samp'}, use_global_device_ids=true, to_apply=%region_8.9 | all-reduce | flops 128 | bytes 1024 | tf_op jit(solution)/shard_map/pmax | solution.py:54
  150.4 0.2 exponential_reduce_fusion
  150.5 36.6 %psum.15 = f32[128]{0:T(128)S(1)} all-reduce(f32[128]{0:T(128)S(1)} %exponential_reduce_fusion), channel_id=1, replica_groups=mesh['samp'=16,'tp'=2] {'samp'}, use_global_device_ids=true, to_apply=%region_10.11 | all-reduce | flops 128 | bytes 1024 | tf_op jit(solution)/shard_map/psum | solution.py:55
  187.1 0.5 fusion.19
  187.6 0.1 subtract_add_fusion
  187.7 0.7 copy.15
  (18 shorter events, 0.4 us)
Async XLA Ops:
  9.0 97.7 %copy-start = (f32[128,8,128]{2,1,0:T(8,128)S(1)}, f32[128,8,128]{2,1,0:T(8,128)}, u32[]{:S(2)}) copy-start(f32[128,8,128]{2,1,0:T(8,128)} %param.14) | copy-start | bytes 1572868
  9.0 97.7 %copy-start.1 = (f32[128,128]{1,0:T(8,128)S(1)}, f32[128,128]{1,0:T(8,128)}, u32[]{:S(2)}) copy-start(f32[128,128]{1,0:T(8,128)} %param.12) | copy-start | bytes 196612
  9.0 97.7 %copy-start.2 = (f32[128,128]{1,0:T(8,128)S(1)}, f32[128,128]{1,0:T(8,128)}, u32[]{:S(2)}) copy-start(f32[128,128]{1,0:T(8,128)} %param.13) | copy-start | bytes 196612
where the time goes:
time: 189 us; the launch traced here: 188 us
  blocking collectives  87.8 us (46%)
  local copies, waits for them, and re-layouts  53 us (28%)
  matrix products  37.1 us (20%)
  other arithmetic  8.71 us (5%)
    sub x12, local copies, waits for them, and re-layouts, add_piece(): image_piece[:, None, :].astype(jnp.float32) - pixel_mean  46.8 us
    pmax x1, blocking collectives, on_device(): peak = lax.pmax(local_peak, 'samp')  43.2 us
    psum x1, blocking collectives, on_device(): sum_exp = lax.psum(jnp.sum(jnp.exp(logw - peak[:, None]), axis=1), 'samp')  36.6 us
    dot_general x6, matrix products, add_piece(): jnp.dot(hidden, w_piece, preferred_element_type=jnp.float32) + bias_piece  35.4 us
    convert_element_type x6, other arithmetic, add_piece(): image_piece[:, None, :].astype(jnp.float32) - pixel_mean  5.94 us
    dynamic_slice x6, local copies, waits for them, and re-layouts, add_piece(): inverse_piece = lax.dynamic_slice_in_dim(inverse, offset, piece_width, 1)  4.22 us

commit v1 on v0

v1 whole, which is shorter than its diff:
```python
import functools
import math

import jax
import jax.numpy as jnp
from jax import lax
from jax.experimental import pallas as pl
from jax.experimental.pallas import tpu as pltpu
from jax.sharding import PartitionSpec as P

HALF_LOG_TAU = 0.9189385332046727


def decoder_kernel(
    row_chunk,
    tp_size,
    noise_ref,
    mean_ref,
    logscale_ref,
    w_in_ref,
    b_in_ref,
    w_ref,
    bias_ref,
    pixel_logscale_ref,
    image_ref,
    whole_logscale_ref,
    out_ref,
    hidden_ref,
    squares_ref,
    latent_terms_ref,
):
    step = pl.program_id(0)
    images, samples, latent_dims = noise_ref.shape
    rows = images * samples
    width = w_ref.shape[1]

    @pl.when(step == 0)
    def _():
        noise = noise_ref[...]
        logscale = logscale_ref[...][:, None, :]
        latent = mean_ref[...][:, None, :] + jnp.exp(logscale) * noise
        latent_terms_ref[...] = (
            (-0.5 * latent * latent) - (-0.5 * noise * noise - logscale)
        ) * (1.0 / tp_size)
        squares_ref[...] = jnp.zeros_like(squares_ref)
        latent_rows = latent.reshape(rows, latent_dims).astype(jnp.bfloat16)
        hidden = jnp.dot(latent_rows, w_in_ref[...], preferred_element_type=jnp.float32)
        hidden = hidden + b_in_ref[...].astype(jnp.float32)
        hidden_ref[...] = jnp.maximum(hidden, 0.0).astype(jnp.bfloat16)

    inverse = jnp.exp(-pixel_logscale_ref[...])
    target = (image_ref[...].astype(jnp.float32) - bias_ref[...]) * inverse
    image_chunk = row_chunk // samples
    for at in range(0, rows, row_chunk):
        first = at // samples
        mean = jnp.dot(
            hidden_ref[at : at + row_chunk, :], w_ref[...], preferred_element_type=jnp.float32
        ).reshape(image_chunk, samples, width)
        scaled = target[first : first + image_chunk, None, :] - mean * inverse[None]
        square = scaled * scaled
        folded = square[:, :, :128]
        for lane in range(128, width, 128):
            folded = folded + square[:, :, lane : lane + 128]
        squares_ref[first : first + image_chunk] += folded

    @pl.when(step == pl.num_programs(0) - 1)
    def _():
        constant = -jnp.sum(whole_logscale_ref[...]) - whole_logscale_ref.shape[1] * HALF_LOG_TAU
        terms = latent_terms_ref[...] - 0.5 * squares_ref[...]
        sums = jnp.sum(terms, axis=2, keepdims=True)
        image_at = lax.broadcasted_iota(jnp.int32, (images, samples, images), 0)
        lane_at = lax.broadcasted_iota(jnp.int32, (images, samples, images), 2)
        placed = jnp.sum(jnp.where(image_at == lane_at, sums, 0.0), axis=0) + constant
        out_ref[...] = jnp.broadcast_to(placed[None], out_ref.shape)


def finish_kernel(samp_axis, tp_size, all_pixels, received_ref, bound_ref, weights_ref):
    samp_size = received_ref.shape[0] // tp_size
    samples = received_ref.shape[1]
    all_samples = samp_size * samples
    parts = received_ref[...].reshape(samp_size, tp_size, *received_ref.shape[1:])
    logw = parts[:, 0]
    for half in range(1, tp_size):
        logw = logw + parts[:, half]
    peak = jnp.max(jnp.max(logw, axis=0), axis=0, keepdims=True)
    sum_exp = jnp.sum(jnp.sum(jnp.exp(logw - peak[None]), axis=0), axis=0, keepdims=True)
    log_sum = jnp.log(sum_exp)
    log_count = math.log(all_samples)
    bound_ref[...] = (peak + log_sum - log_count) / all_pixels
    me = lax.axis_index(samp_axis)
    own = received_ref[pl.ds(me * tp_size, tp_size)]
    mine = own[0]
    for half in range(1, tp_size):
        mine = mine + own[half]
    weights_ref[...] = (mine - peak) - log_sum + log_count


def on_device(
    mesh_shape, images, enc_mean, enc_logscale, noise, w_in, b_in, w_out, b_out, pixel_logscale
):
    samp_size, tp_size = mesh_shape["samp"], mesh_shape["tp"]
    devices = samp_size * tp_size
    image_count, sample_count, latent_dims = noise.shape
    rows = image_count * sample_count
    hidden_units = w_out.shape[0]
    share = images.shape[1]
    width = math.gcd(share, 1024)
    w_whole, b_whole = (
        lax.all_gather(w_in, "tp", axis=1, tiled=True),
        lax.all_gather(b_in, "tp", axis=1, tiled=True),
    )
    whole = lambda shape: pl.BlockSpec(shape, lambda j: (0,) * len(shape))
    columns = lambda count: pl.BlockSpec((count, width), lambda j: (0, j))
    partial = pl.pallas_call(
        functools.partial(decoder_kernel, math.gcd(rows, 256), tp_size),
        grid=(share // width,),
        in_specs=[
            whole(noise.shape),
            whole(enc_mean.shape),
            whole(enc_logscale.shape),
            whole(w_whole.shape),
            whole(b_whole.shape),
            columns(hidden_units),
            columns(1),
            columns(1),
            columns(image_count),
            whole(pixel_logscale.shape),
        ],
        out_specs=whole((devices, sample_count, image_count)),
        out_shape=jax.ShapeDtypeStruct((devices, sample_count, image_count), jnp.float32),
        scratch_shapes=[
            pltpu.VMEM((rows, hidden_units), jnp.bfloat16),
            pltpu.VMEM((image_count, sample_count, 128), jnp.float32),
            pltpu.VMEM((image_count, sample_count, latent_dims), jnp.float32),
        ],
        cost_estimate=pl.CostEstimate(
            flops=2 * rows * hidden_units * (share + latent_dims),
            bytes_accessed=2 * hidden_units * share + 2 * image_count * share + 4 * rows * latent_dims,
            transcendentals=share,
        ),
        name="decoder",
    )(
        noise,
        enc_mean,
        enc_logscale,
        w_whole,
        b_whole,
        w_out,
        b_out,
        pixel_logscale,
        images,
        pixel_logscale,
    )
    received = lax.all_to_all(partial, ("samp", "tp"), 0, 0)
    bound, weights = pl.pallas_call(
        functools.partial(finish_kernel, "samp", tp_size, share * tp_size),
        out_shape=(
            jax.ShapeDtypeStruct((1, image_count), jnp.float32),
            jax.ShapeDtypeStruct((sample_count, image_count), jnp.float32),
        ),
        name="finish",
    )(received)
    return bound.reshape(image_count), weights.T


def solution(mesh):
    in_specs = (
        P(None, "tp"),
        P(),
        P(),
        P(None, "samp", None),
        P(None, "tp"),
        P(None, "tp"),
        P(None, "tp"),
        P(None, "tp"),
        P(None, "tp"),
    )
    out_specs = (P(), P(None, "samp"))
    return jax.shard_map(
        functools.partial(on_device, dict(mesh.shape)),
        mesh=mesh,
        in_specs=in_specs,
        out_specs=out_specs,
        check_vma=False,
    )
```

time: 189 us -> 44.7 us (0.24)
  blocking collectives: 87.8 us -> 22.5 us
  local copies, waits for them, and re-layouts: 53 us -> 0 us
  matrix products: 37.1 us -> 0 us
  Pallas kernels: 0 us -> 21.3 us
  other arithmetic: 8.71 us -> 0 us
    sub x12 -> x0, local copies, waits for them, and re-layouts: 46.8 us -> none  [add_piece(): image_piece[:, None, :].astype(jnp.float32) - pixel_mean]
    pmax x1 -> x0, blocking collectives: 43.2 us -> none  [on_device(): peak = lax.pmax(local_peak, 'samp')]
    psum x2 -> x0, blocking collectives: 40.3 us -> none  [the longest x1 36.6 us: on_device(): sum_exp = lax.psum(jnp.sum(jnp.exp(logw - peak[:, None]), axis=1), 'samp')]
    dot_general x7 -> x0, matrix products: 37.1 us -> none  [the longest x6 35.4 us: add_piece(): jnp.dot(hidden, w_piece, preferred_element_type=jnp.float32) + bias_piece]
    pallas_call x0 -> x2, Pallas kernels: none -> 21.3 us  [the longest x1 19.8 us: on_device(): pl.pallas_call(functools.partial(decoder_kernel, math.gcd(rows, 256), tp_...]
    all_to_all x0 -> x1, blocking collectives: none -> 15.5 us  [on_device(): received = lax.all_to_all(partial, ('samp', 'tp'), 0, 0)]
    convert_element_type x6 -> x0, other arithmetic: 5.94 us -> none  [add_piece(): image_piece[:, None, :].astype(jnp.float32) - pixel_mean]
    dynamic_slice x6 -> x0, local copies, waits for them, and re-layouts: 4.22 us -> none  [add_piece(): inverse_piece = lax.dynamic_slice_in_dim(inverse, offset, piece_width, 1)]
where the time goes in v1:
time: 44.7 us; the launch traced here: 44.4 us
  blocking collectives  22.5 us (50%)
  Pallas kernels  21.3 us (48%)
  between operations  0.63 us (1%)
    pallas_call x1, Pallas kernels, on_device(): pl.pallas_call(functools.partial(decoder_kernel, math.gcd(rows, 256), tp_...  19.8 us
    all_to_all x1, blocking collectives, on_device(): received = lax.all_to_all(partial, ('samp', 'tp'), 0, 0)  15.5 us
    all_gather x1, blocking collectives, on_device(): lax.all_gather(w_in, 'tp', axis=1, tiled=True)  3.55 us
    all_gather x1, blocking collectives, on_device(): lax.all_gather(b_in, 'tp', axis=1, tiled=True)  3.42 us
    pallas_call x1, Pallas kernels, on_device(): pl.pallas_call(functools.partial(finish_kernel, 'samp', tp_size, share *...  1.55 us

profile of v1, /device:TPU:0, one launch (start us, length us, event | category | flops | bytes accessed | tf_op | source)
XLA Modules:
  0.0 44.4 jit_solution(14340173150441802975)
XLA Ops:
  0.6 3.4 %all_gather.7.b_in_ref = bf16[1,1024]{1,0:T(2,128)(2,1)} all-gather(bf16[1,512]{1,0:T(2,128)(2,1)} %param.14), channel_id=1, replica_groups=mesh['samp'=16,'tp'=2] {'tp'}, dimensions={1}, use_global_device_ids=true | all-gather | bytes 3072 | tf_op jit(solution)/shard_map/all_gather | solution.py:110
  4.0 3.5 %all_gather.6.w_in_ref = bf16[128,1024]{1,0:T(8,128)(2,1)} all-gather(bf16[128,512]{1,0:T(8,128)(2,1)} %param.13), channel_id=1, replica_groups=mesh['samp'=16,'tp'=2] {'tp'}, dimensions={1}, use_global_device_ids=true | all-gather | bytes 393216 | tf_op jit(solution)/shard_map/all_gather | solution.py:109
  7.6 19.8 %decoder.1 = f32[32,8,128]{2,1,0:T(8,128)} custom-call(f32[128,8,128]{2,1,0:T(8,128)} %noise_ref.1, f32[128,128]{1,0:T(8,128)} %mean_ref.1, f32[128,128]{1,0:T(8,128)} %logscale_ref.1, bf16[128,1024]{1,0:T(8,128)(2,1)} %all_gather.6.w_in_ref, bf16[1,1024]{1,0:T(2,128)(2,1)} %all_gather.7.b_in_ref, bf16[1024,6144]{1,0:T(8,128)(2,1)} %w_ref.1, ...), custom_call_target="tpu_custom_call" | custom-call | flops 13153337344 | bytes 14680064 | tf_op jit(solution)/shard_map/decoder/pallas_call | solution.py:114
  27.4 15.5 %all_to_all.5.received_ref = f32[32,8,128]{2,1,0:T(8,128)} all-to-all(f32[32,8,128]{2,1,0:T(8,128)} %decoder.1), channel_id=1, replica_groups=mesh['samp'=16,'tp'=2] {'samp','tp'}, dimensions={0} | all-to-all | bytes 262144 | tf_op jit(solution)/shard_map/all_to_all | solution.py:154
  42.9 1.6 %finish.1 = (f32[1,128]{1,0:T(1,128)}, f32[8,128]{1,0:T(8,128)}) custom-call(f32[32,8,128]{2,1,0:T(8,128)} %all_to_all.5.received_ref), custom_call_target="tpu_custom_call" | custom-call | tf_op jit(solution)/shard_map/finish/pallas_call | solution.py:155

commit v2 on v1

v2 whole, which is shorter than its diff:
```python
import functools
import math

import jax
import jax.numpy as jnp
from jax import lax
from jax.experimental import pallas as pl
from jax.experimental.pallas import tpu as pltpu
from jax.sharding import PartitionSpec as P

HALF_LOG_TAU = 0.9189385332046727
TILE = 256
LANES = 128


def w_block(w_hbm, target, sem, tp_axis, tp_size, block):
    units, width = w_hbm.shape[0] // tp_size, target.shape[1]
    me = lax.axis_index(tp_axis)
    copies = []
    for part in range(tp_size):
        owner = lax.rem(me + tp_size - part, tp_size)
        copies.append(
            pltpu.make_async_copy(
                w_hbm.at[
                    pl.ds(pl.multiple_of(owner * units, units), units),
                    pl.ds(pl.multiple_of(block * width, width), width),
                ],
                target.at[pl.ds(part * units, units), :],
                sem.at[part],
            )
        )
    return copies


def prepare_kernel(
    tp_axis,
    tp_size,
    noise_hbm,
    mean_hbm,
    logscale_hbm,
    w_in_hbm,
    b_in_hbm,
    bias_hbm,
    pixel_logscale_hbm,
    image_hbm,
    w_hbm,
    latent_ref,
    hidden_ref,
    prior_ref,
    target_ref,
    inverse_ref,
    head_ref,
    noise_ref,
    mean_ref,
    logscale_ref,
    w_in_ref,
    b_in_ref,
    bias_ref,
    pixel_logscale_ref,
    image_ref,
    sem,
    head_sem,
):
    samples, images, latent_dims = noise_ref.shape
    blocks, _, width = target_ref.shape
    pairs = [(noise_hbm.at[:, s, :], noise_ref.at[s]) for s in range(samples)] + [
        (mean_hbm, mean_ref),
        (logscale_hbm, logscale_ref),
        (w_in_hbm, w_in_ref),
        (b_in_hbm, b_in_ref),
        (pixel_logscale_hbm, pixel_logscale_ref),
        (bias_hbm, bias_ref),
        (image_hbm, image_ref),
    ]
    copies = [pltpu.make_async_copy(a, b, sem.at[i]) for i, (a, b) in enumerate(pairs)]
    head = w_block(w_hbm, head_ref.at[0], head_sem, tp_axis, tp_size, 0)
    for copy in copies + head:
        copy.start()
    for copy in copies[: samples + 5]:
        copy.wait()

    latent_ref[:, latent_dims:] = jnp.zeros(
        (samples * images, TILE - latent_dims), jnp.bfloat16
    )
    logscale = logscale_ref[...]
    scale = jnp.exp(logscale)
    constant = (
        -jnp.sum(pixel_logscale_ref[...]) - pixel_logscale_ref.shape[1] * HALF_LOG_TAU
    )
    for s in range(samples):
        rows = slice(s * images, (s + 1) * images)
        noise = noise_ref[s]
        latent = mean_ref[...] + scale * noise
        terms = ((-0.5 * latent * latent) - (-0.5 * noise * noise - logscale)) * (
            1.0 / tp_size
        )
        prior_ref[s : s + 1, :] = jnp.sum(terms.T, axis=0, keepdims=True) + constant
        latent_b = latent.astype(jnp.bfloat16)
        latent_ref[rows, :latent_dims] = latent_b
        own = jnp.dot(latent_b, w_in_ref[...], preferred_element_type=jnp.float32)
        own = own + b_in_ref[...].astype(jnp.float32)
        hidden_ref[rows, :] = jnp.maximum(own, 0.0).astype(jnp.bfloat16)
    inverse_ref[...] = jnp.broadcast_to(
        jnp.exp(-pixel_logscale_ref[...]), inverse_ref.shape
    )
    for copy in copies[samples + 5 :]:
        copy.wait()
    for block in range(blocks):
        columns = slice(block * width, (block + 1) * width)
        target_ref[block] = (
            image_ref[:, columns].astype(jnp.float32) - bias_ref[:, columns]
        ) * inverse_ref[:1, columns]
    for copy in head:
        copy.wait()


def decoder_kernel(
    tp_axis,
    tp_size,
    latent_ref,
    own_ref,
    prior_ref,
    target_ref,
    inverse_ref,
    head_ref,
    *refs,
):
    w_in_refs, b_in_refs = refs[: tp_size - 1], refs[tp_size - 1 : 2 * tp_size - 2]
    w_hbm, out_ref, hidden_ref, w_ref, squares_ref, w_in_pad_ref, sem = refs[2 * tp_size - 2 :]
    blocks, images, width = target_ref.shape
    samples = squares_ref.shape[0]
    units = own_ref.shape[1]
    latent_dims = w_in_refs[0].shape[0]
    depth = w_hbm.shape[0] // TILE

    def w_copies(block):
        return w_block(w_hbm, w_ref.at[block - 1], sem.at[block - 1], tp_axis, tp_size, block)

    for block in range(1, blocks):
        for copy in w_copies(block):
            copy.start()

    def body(*accs):
        acc = (accs[:samples], accs[samples:])
        rows = [slice(s * images, (s + 1) * images) for s in range(samples)]
        for q in range(2):
            for s in range(samples):
                pltpu.matmul_pop(acc[q][s])

        for part in range(1, tp_size):
            w_in_pad_ref[:latent_dims, :] = w_in_refs[part - 1][...]
            w_in_pad_ref[latent_dims:, :] = jnp.zeros(
                (TILE - latent_dims, units), jnp.bfloat16
            )
            for tile in range(0, units // TILE, 2):
                for q in range(2):
                    at = (tile + q) * TILE
                    pltpu.matmul_push_rhs(
                        w_in_pad_ref[:, at : at + TILE], staging_register=1, mxu_index=q
                    )
                for s in range(samples):
                    for q in range(2):
                        pltpu.matmul_acc_lhs(
                            acc[q][s],
                            latent_ref[rows[s], :],
                            load_staged_rhs=1 if s == 0 else None,
                        )
                for s in range(samples):
                    for q in range(2):
                        at = (tile + q) * TILE
                        bias = b_in_refs[part - 1][:, at : at + TILE].astype(jnp.float32)
                        unit = jnp.maximum(pltpu.matmul_pop(acc[q][s]) + bias, 0.0)
                        at += (part - 1) * units
                        hidden_ref[rows[s], at : at + TILE] = unit.astype(jnp.bfloat16)

        def lhs(s, k):
            at = k * TILE
            if at < units:
                return own_ref[rows[s], at : at + TILE]
            return hidden_ref[rows[s], at - units : at - units + TILE]

        def push(block, k, register):
            for q in range(2):
                deep, wide = slice(k * TILE, (k + 1) * TILE), slice(q * TILE, (q + 1) * TILE)
                if isinstance(block, int) and block == 0:
                    tile = head_ref[0, deep, wide]
                else:
                    tile = w_ref[block - 1, deep, wide]
                pltpu.matmul_push_rhs(tile, staging_register=register, mxu_index=q)

        def take(block, s):
            total = squares_ref[s]
            for q in range(2):
                product = pltpu.matmul_pop(acc[q][s]).reshape(images // 8, 8, TILE)
                at = block * width + q * TILE
                if not isinstance(block, int):
                    at = pl.multiple_of(at, TILE)
                inverse = inverse_ref[:, pl.ds(at, TILE)]
                target = target_ref[block, :, q * TILE : (q + 1) * TILE]
                scaled = target.reshape(images // 8, 8, TILE) - product * inverse[None]
                square = (scaled * scaled).reshape(images, TILE)
                for lane in range(0, TILE, LANES):
                    total = total + square[:, lane : lane + LANES]
            squares_ref[s] = total

        first, second = range(samples // 2), range(samples // 2, samples)

        def half(block, mine, following, taken, done):
            for k in range(depth):
                for index, s in enumerate(mine):
                    for q in range(2):
                        pltpu.matmul_acc_lhs(
                            acc[q][s], lhs(s, k), load_staged_rhs=k % 2 if index == 0 else None
                        )
                    if index == 0:
                        if k + 1 < depth:
                            push(block, k + 1, (k + 1) % 2)
                        elif following is not None:
                            push(following, 0, 0)
                count = len(done)
                for s in done[k * count // depth : (k + 1) * count // depth]:
                    take(taken, s)

        def block_step(block):
            for copy in w_copies(block + 1):
                copy.wait()
            half(block, second, block + 1, block, first)
            half(block + 1, first, block + 1, block, second)

        squares_ref[...] = jnp.zeros_like(squares_ref)
        push(0, 0, 0)
        half(0, first, 0, None, ())
        block_step(0)

        @pl.loop(1, blocks - 1)
        def _(block):
            block_step(block)

        half(blocks - 1, second, None, blocks - 1, first)
        for s in second:
            take(blocks - 1, s)

        for s in range(samples):
            row = prior_ref[s : s + 1, :] - 0.5 * jnp.sum(
                squares_ref[s].T, axis=0, keepdims=True
            )
            out_ref[:, s, :] = jnp.broadcast_to(row, (out_ref.shape[0], images))

    pl.run_scoped(
        body,
        *[
            pltpu.ACC(q)((images, TILE), jnp.float32)
            for q in range(2)
            for _ in range(samples)
        ],
    )


def finish_kernel(samp_axis, tp_size, all_pixels, received_ref, bound_ref, weights_ref):
    samp_size = received_ref.shape[0] // tp_size
    samples = received_ref.shape[1]
    all_samples = samp_size * samples
    parts = received_ref[...].reshape(samp_size, tp_size, *received_ref.shape[1:])
    logw = parts[:, 0]
    for half in range(1, tp_size):
        logw = logw + parts[:, half]
    peak = jnp.max(jnp.max(logw, axis=0), axis=0, keepdims=True)
    sum_exp = jnp.sum(jnp.sum(jnp.exp(logw - peak[None]), axis=0), axis=0, keepdims=True)
    log_sum = jnp.log(sum_exp)
    log_count = math.log(all_samples)
    bound_ref[...] = (peak + log_sum - log_count) / all_pixels
    me = lax.axis_index(samp_axis)
    own = received_ref[pl.ds(me * tp_size, tp_size)]
    mine = own[0]
    for half in range(1, tp_size):
        mine = mine + own[half]
    weights_ref[...] = (mine - peak) - log_sum + log_count


def on_device(
    mesh_shape, images, enc_mean, enc_logscale, noise, w_in, b_in, w_out, b_out, pixel_logscale
):
    samp_size, tp_size = mesh_shape["samp"], mesh_shape["tp"]
    devices = samp_size * tp_size
    image_count, sample_count, latent_dims = noise.shape
    rows = image_count * sample_count
    units = w_in.shape[1]
    hidden_units, pixels = w_out.shape
    width = 2 * TILE
    blocks = pixels // width

    def from_neighbour(value, shift):
        return lax.ppermute(
            value, "tp", [(a, (a + shift) % tp_size) for a in range(tp_size)]
        )

    w_in_others = [from_neighbour(w_in, shift) for shift in range(1, tp_size)]
    b_in_others = [from_neighbour(b_in, shift) for shift in range(1, tp_size)]
    hbm = pl.BlockSpec(memory_space=pltpu.HBM)
    vmem = pl.BlockSpec(memory_space=pltpu.VMEM)
    f32, bf16 = jnp.float32, jnp.bfloat16
    in_hbm = lambda value: pltpu.with_memory_space_constraint(value, pltpu.HBM)
    prepared = pl.pallas_call(
        functools.partial(prepare_kernel, "tp", tp_size),
        in_specs=[hbm] * 9,
        out_specs=[vmem] * 6,
        out_shape=[
            jax.ShapeDtypeStruct((rows, TILE), bf16),
            jax.ShapeDtypeStruct((rows, units), bf16),
            jax.ShapeDtypeStruct((sample_count, image_count), f32),
            jax.ShapeDtypeStruct((blocks, image_count, width), f32),
            jax.ShapeDtypeStruct((8, pixels), f32),
            jax.ShapeDtypeStruct((1, hidden_units, width), bf16),
        ],
        scratch_shapes=[
            pltpu.VMEM((sample_count, image_count, latent_dims), f32),
            pltpu.VMEM(enc_mean.shape, f32),
            pltpu.VMEM(enc_logscale.shape, f32),
            pltpu.VMEM(w_in.shape, bf16),
            pltpu.VMEM(b_in.shape, bf16),
            pltpu.VMEM(b_out.shape, f32),
            pltpu.VMEM(pixel_logscale.shape, f32),
            pltpu.VMEM(images.shape, bf16),
            pltpu.SemaphoreType.DMA((sample_count + 7,)),
            pltpu.SemaphoreType.DMA((tp_size,)),
        ],
        compiler_params=pltpu.CompilerParams(vmem_limit_bytes=14 << 20),
        cost_estimate=pl.CostEstimate(
            flops=2 * rows * latent_dims * units + 20 * image_count * pixels,
            bytes_accessed=2 * image_count * pixels + 4 * rows * latent_dims,
            transcendentals=pixels,
        ),
        name="prepare",
    )(*map(in_hbm, (noise, enc_mean, enc_logscale, w_in, b_in, b_out, pixel_logscale, images, w_out)))
    partial = pl.pallas_call(
        functools.partial(decoder_kernel, "tp", tp_size),
        in_specs=[vmem] * (6 + 2 * (tp_size - 1)) + [hbm],
        out_specs=vmem,
        out_shape=jax.ShapeDtypeStruct((devices, sample_count, image_count), f32),
        scratch_shapes=[
            pltpu.VMEM((rows, hidden_units - units), bf16),
            pltpu.VMEM((blocks - 1, hidden_units, width), bf16),
            pltpu.VMEM((sample_count, image_count, LANES), f32),
            pltpu.VMEM((TILE, units), bf16),
            pltpu.SemaphoreType.DMA((blocks - 1, tp_size)),
        ],
        compiler_params=pltpu.CompilerParams(vmem_limit_bytes=32 << 20),
        cost_estimate=pl.CostEstimate(
            flops=2 * rows * hidden_units * pixels,
            bytes_accessed=2 * hidden_units * pixels,
            transcendentals=0,
        ),
        name="decoder",
    )(*prepared, *w_in_others, *b_in_others, in_hbm(w_out))
    received = lax.all_to_all(partial, ("samp", "tp"), 0, 0)
    bound, weights = pl.pallas_call(
        functools.partial(finish_kernel, "samp", tp_size, pixels * tp_size),
        in_specs=[vmem],
        out_shape=(
            jax.ShapeDtypeStruct((1, image_count), f32),
            jax.ShapeDtypeStruct((sample_count, image_count), f32),
        ),
        compiler_params=pltpu.CompilerParams(vmem_limit_bytes=4 << 20),
        name="finish",
    )(received)
    return bound.reshape(image_count), weights.T


def solution(mesh):
    in_specs = (
        P(None, "tp"),
        P(),
        P(),
        P(None, "samp", None),
        P(None, "tp"),
        P(None, "tp"),
        P(None, "tp"),
        P(None, "tp"),
        P(None, "tp"),
    )
    out_specs = (P(), P(None, "samp"))
    return jax.shard_map(
        functools.partial(on_device, dict(mesh.shape)),
        mesh=mesh,
        in_specs=in_specs,
        out_specs=out_specs,
        check_vma=False,
    )
```

time: 44.7 us -> 35.3 us (0.79)
  blocking collectives: 22.5 us -> 15.3 us
  Pallas kernels: 21.3 us -> 18.6 us
  starting transfers between devices: 0 us -> 0.64 us
    all_gather x2 -> x0, blocking collectives: 6.96 us -> none  [the longest x1 3.55 us: on_device(): lax.all_gather(w_in, 'tp', axis=1, tiled=True)]
    pallas_call x2 -> x3, Pallas kernels: 21.3 us -> 18.6 us  [the longest x1 15.7 us: on_device(): pl.pallas_call(functools.partial(decoder_kernel, 'tp', tp_size), in_specs...]
    ppermute x0 -> x2, starting transfers between devices: none -> 0.64 us  [from_neighbour(): lax.ppermute(value, 'tp', [(a, (a + shift) % tp_size) for a in range(tp_s...]
  transfers between devices with their start and end apart: 0 -> 2, of which waited for: 0 -> 0; matrix products, arithmetic and copies ran while one was open for 0% -> 0% of each run, Pallas kernels for 0% -> 6%
where the time goes in v2:
time: 35.3 us; the launch traced here: 35.2 us
  Pallas kernels  18.6 us (53%)
  blocking collectives  15.3 us (43%)
  between operations  0.67 us (2%)
  starting transfers between devices  0.64 us (2%)
    pallas_call x1, Pallas kernels, on_device(): pl.pallas_call(functools.partial(decoder_kernel, 'tp', tp_size), in_specs...  15.7 us
    all_to_all x1, blocking collectives, on_device(): received = lax.all_to_all(partial, ('samp', 'tp'), 0, 0)  15.3 us
    pallas_call x1, Pallas kernels, on_device(): pl.pallas_call(functools.partial(prepare_kernel, 'tp', tp_size), in_specs...  2.25 us
  transfers between devices with their start and end apart: 2, of which 0 were waited for; matrix products, arithmetic and copies ran while one was open for 0% of the time, Pallas kernels for 6%

profile of v2, /device:TPU:0, one launch (start us, length us, event | category | flops | bytes accessed | tf_op | source)
XLA Modules:
  0.0 35.2 jit_solution(10777087267978511230)
XLA Ops:
  0.6 0.6 %collective-permute-start = (bf16[128,512]{1,0:T(8,128)(2,1)}, bf16[128,512]{1,0:T(8,128)(2,1)S(1)}, u32[]{:S(2)}, u32[]{:S(2)}) collective-permute-start(bf16[128,512]{1,0:T(8,128)(2,1)} %w_in_hbm.1), channel_id=1, source_target_pairs={{0,1},{1,0},{2,3},{3,2},{4,5},{5,4},{6,7},{7,6},{8,9},{9,8},{10,11... | collective-permute-start | bytes 393224 | tf_op jit(solution)/shard_map/ppermute | solution.py:293
  1.2 0.1 collective-permute-start.1
  1.3 2.2 %prepare.1 = (bf16[1024,256]{1,0:T(8,128)(2,1)S(1)}, bf16[1024,512]{1,0:T(8,128)(2,1)S(1)}, f32[8,128]{1,0:T(8,128)S(1)}, f32[12,128,512]{2,1,0:T(8,128)S(1)}, f...) custom-call(f32[128,8,128]{2,1,0:T(8,128)} %noise_hbm.1, f32[128,128]{1,0:T(8,128)} %mean_hbm.1, ...), custom_call_target="tpu_custom_call" | custom-call | flops 149946368 | bytes 2097152 | tf_op jit(solution)/shard_map/prepare/pallas_call | solution.py:303
  3.5 0.0 collective-permute-done.1.refs_1_
  3.5 0.0 collective-permute-done.refs_0_
  3.5 15.7 %decoder.1 = f32[32,8,128]{2,1,0:T(8,128)S(1)} custom-call(bf16[1024,256]{1,0:T(8,128)(2,1)S(1)} %get-tuple-element.10.latent_ref, bf16[1024,512]{1,0:T(8,128)(2,1)S(1)} %get-tuple-element.11.own_ref, f32[8,128]{1,0:T(8,128)S(1)} %get-tuple-element.12.prior_ref, f32[12,128,512]{2,1,0:T(8,128)S(1)} %get-tuple-element.13.target_ref, ...), custom_call_target="tpu_custom_call" | custom-call | flops 12884901888 | bytes 12582912 | tf_op jit(solution)/shard_map/decoder/pallas_call | solution.py:335
  19.2 15.3 %all_to_all.5.received_ref = f32[32,8,128]{2,1,0:T(8,128)S(1)} all-to-all(f32[32,8,128]{2,1,0:T(8,128)S(1)} %decoder.1), channel_id=1, replica_groups=mesh['samp'=16,'tp'=2] {'samp','tp'}, dimensions={0} | all-to-all | bytes 262144 | tf_op jit(solution)/shard_map/all_to_all | solution.py:355
  34.5 0.6 %finish.1 = (f32[1,128]{1,0:T(1,128)}, f32[8,128]{1,0:T(8,128)}) custom-call(f32[32,8,128]{2,1,0:T(8,128)S(1)} %all_to_all.5.received_ref), custom_call_target="tpu_custom_call" | custom-call | tf_op jit(solution)/shard_map/finish/pallas_call | solution.py:356
Async XLA Ops:
  0.6 2.9 %collective-permute-start = (bf16[128,512]{1,0:T(8,128)(2,1)}, bf16[128,512]{1,0:T(8,128)(2,1)S(1)}, u32[]{:S(2)}, u32[]{:S(2)}) collective-permute-start(bf16[128,512]{1,0:T(8,128)(2,1)} %w_in_hbm.1), channel_id=1, source_target_pairs={{0,1},{1,0},{2,3},{3,2},{4,5},{5,4},{6,7},{7,6},{8,9},{9,8},{10,11... | collective-permute-start | bytes 393224 | tf_op jit(solution)/shard_map/ppermute | solution.py:293
  1.2 2.3 %collective-permute-start.1 = (bf16[1,512]{1,0:T(2,128)(2,1)}, bf16[1,512]{1,0:T(2,128)(2,1)S(1)}, u32[]{:S(2)}, u32[]{:S(2)}) collective-permute-start(bf16[1,512]{1,0:T(2,128)(2,1)} %b_in_hbm.1), channel_id=1, source_target_pairs={{0,1},{1,0},{2,3},{3,2},{4,5},{5,4},{6,7},{7,6},{8,9},{9,8},{10,11... | collective-permute-start | bytes 3080 | tf_op jit(solution)/shard_map/ppermute | solution.py:293

commit v3 on v2

--- a/solution.py
+++ b/solution.py
@@ -10,6 +10,7 @@
 
 HALF_LOG_TAU = 0.9189385332046727
 TILE = 256
+AHEAD = 2
 LANES = 128
 
 
@@ -49,20 +50,20 @@
     prior_ref,
     target_ref,
     inverse_ref,
+    bias_ref,
     head_ref,
     noise_ref,
     mean_ref,
     logscale_ref,
     w_in_ref,
     b_in_ref,
-    bias_ref,
     pixel_logscale_ref,
     image_ref,
     sem,
     head_sem,
 ):
     samples, images, latent_dims = noise_ref.shape
-    blocks, _, width = target_ref.shape
+    heads, _, width = target_ref.shape
     pairs = [(noise_hbm.at[:, s, :], noise_ref.at[s]) for s in range(samples)] + [
         (mean_hbm, mean_ref),
         (logscale_hbm, logscale_ref),
@@ -70,13 +71,17 @@
         (b_in_hbm, b_in_ref),
         (pixel_logscale_hbm, pixel_logscale_ref),
         (bias_hbm, bias_ref),
-        (image_hbm, image_ref),
+        (image_hbm.at[:, pl.ds(0, heads * width)], image_ref),
     ]
     copies = [pltpu.make_async_copy(a, b, sem.at[i]) for i, (a, b) in enumerate(pairs)]
-    head = w_block(w_hbm, head_ref.at[0], head_sem, tp_axis, tp_size, 0)
+    head = []
+    for block in range(heads):
+        head += w_block(
+            w_hbm, head_ref.at[block], head_sem.at[block], tp_axis, tp_size, block
+        )
     for copy in copies + head:
         copy.start()
-    for copy in copies[: samples + 5]:
+    for copy in copies[: samples + 2]:
         copy.wait()
 
     latent_ref[:, latent_dims:] = jnp.zeros(
@@ -84,6 +89,8 @@
     )
     logscale = logscale_ref[...]
     scale = jnp.exp(logscale)
+    for copy in copies[samples + 2 : samples + 5]:
+        copy.wait()
     constant = (
         -jnp.sum(pixel_logscale_ref[...]) - pixel_logscale_ref.shape[1] * HALF_LOG_TAU
     )
@@ -105,7 +112,7 @@
     )
     for copy in copies[samples + 5 :]:
         copy.wait()
-    for block in range(blocks):
+    for block in range(heads):
         columns = slice(block * width, (block + 1) * width)
         target_ref[block] = (
             image_ref[:, columns].astype(jnp.float32) - bias_ref[:, columns]
@@ -120,25 +127,49 @@
     latent_ref,
     own_ref,
     prior_ref,
-    target_ref,
+    head_target_ref,
     inverse_ref,
+    bias_ref,
     head_ref,
     *refs,
 ):
     w_in_refs, b_in_refs = refs[: tp_size - 1], refs[tp_size - 1 : 2 * tp_size - 2]
-    w_hbm, out_ref, hidden_ref, w_ref, squares_ref, w_in_pad_ref, sem = refs[2 * tp_size - 2 :]
-    blocks, images, width = target_ref.shape
+    (
+        image_hbm,
+        w_hbm,
+        out_ref,
+        hidden_ref,
+        w_ref,
+        image_ref,
+        target_ref,
+        squares_ref,
+        row_ref,
+        w_in_pad_ref,
+        sem,
+        image_sem,
+    ) = refs[2 * tp_size - 2 :]
+    heads, images, width = head_target_ref.shape
+    blocks = heads + w_ref.shape[0]
     samples = squares_ref.shape[0]
     units = own_ref.shape[1]
     latent_dims = w_in_refs[0].shape[0]
     depth = w_hbm.shape[0] // TILE
 
-    def w_copies(block):
-        return w_block(w_hbm, w_ref.at[block - 1], sem.at[block - 1], tp_axis, tp_size, block)
-
-    for block in range(1, blocks):
-        for copy in w_copies(block):
+    def fetches(block):
+        at = block - heads
+        image = pltpu.make_async_copy(
+            image_hbm.at[:, pl.ds(pl.multiple_of(block * width, width), width)],
+            image_ref.at[at], image_sem.at[at]
+        )
+        w_copies = w_block(w_hbm, w_ref.at[at], sem.at[at], tp_axis, tp_size, block)
+        return w_copies + [image]
+
+    def start(block):
+        for copy in fetches(block):
             copy.start()
+
+    for block in range(heads, min(heads + AHEAD, blocks)):
+        start(block)
 
     def body(*accs):
         acc = (accs[:samples], accs[samples:])
@@ -179,34 +210,55 @@
                 return own_ref[rows[s], at : at + TILE]
             return hidden_ref[rows[s], at - units : at - units + TILE]
 
-        def push(block, k, register):
+        def in_head(block):
+            return isinstance(block, int) and block < heads
+
+        def push(block, k):
             for q in range(2):
                 deep, wide = slice(k * TILE, (k + 1) * TILE), slice(q * TILE, (q + 1) * TILE)
-                if isinstance(block, int) and block == 0:
-                    tile = head_ref[0, deep, wide]
+                if in_head(block):
+                    tile = head_ref[block, deep, wide]
                 else:
-                    tile = w_ref[block - 1, deep, wide]
-                pltpu.matmul_push_rhs(tile, staging_register=register, mxu_index=q)
+                    tile = w_ref[block - heads, deep, wide]
+                pltpu.matmul_push_rhs(tile, staging_register=k % 2, mxu_index=q)
+
+        def columns_of(block, first_column, count):
+            at = block * width + first_column
+            return pl.ds(at if isinstance(block, int) else pl.multiple_of(at, count), count)
+
+        def make_target(block):
+            columns = columns_of(block, 0, width)
+            image = image_ref[block - heads].astype(jnp.float32)
+            target_ref[block - heads] = (image - bias_ref[:, columns]) * inverse_ref[:1, columns]
+
+        def finish_row(s, total):
+            lanes = jnp.sum(total.T, axis=0, keepdims=True)
+            row_ref[s : s + 1, :] = prior_ref[s : s + 1, :] - 0.5 * lanes
 
         def take(block, s):
             total = squares_ref[s]
             for q in range(2):
                 product = pltpu.matmul_pop(acc[q][s]).reshape(images // 8, 8, TILE)
-                at = block * width + q * TILE
-                if not isinstance(block, int):
-                    at = pl.multiple_of(at, TILE)
-                inverse = inverse_ref[:, pl.ds(at, TILE)]
-                target = target_ref[block, :, q * TILE : (q + 1) * TILE]
+                inverse = inverse_ref[:, columns_of(block, q * TILE, TILE)]
+                wide = slice(q * TILE, (q + 1) * TILE)
+                if in_head(block):
+                    target = head_target_ref[block, :, wide]
+                else:
+                    target = target_ref[block - heads, :, wide]
                 scaled = target.reshape(images // 8, 8, TILE) - product * inverse[None]
                 square = (scaled * scaled).reshape(images, TILE)
                 for lane in range(0, TILE, LANES):
                     total = total + square[:, lane : lane + LANES]
-            squares_ref[s] = total
-
+            if isinstance(block, int) and block == blocks - 1:
+                finish_row(s, total)
+            else:
+                squares_ref[s] = total
+
+        middle = depth // 2
         first, second = range(samples // 2), range(samples // 2, samples)
 
-        def half(block, mine, following, taken, done):
-            for k in range(depth):
+        def multiply(block, mine, depths, following, taken, done):
+            for k in depths:
                 for index, s in enumerate(mine):
                     for q in range(2):
                         pltpu.matmul_acc_lhs(
@@ -214,37 +266,58 @@
                         )
                     if index == 0:
                         if k + 1 < depth:
-                            push(block, k + 1, (k + 1) % 2)
-                        elif following is not None:
-                            push(following, 0, 0)
+                            push(block, k + 1)
+                        else:
+                            push(following, 0)
                 count = len(done)
                 for s in done[k * count // depth : (k + 1) * count // depth]:
                     take(taken, s)
 
         def block_step(block):
-            for copy in w_copies(block + 1):
-                copy.wait()
-            half(block, second, block + 1, block, first)
-            half(block + 1, first, block + 1, block, second)
+            if not in_head(block + 1):
+                for copy in fetches(block + 1):
+                    copy.wait()
+                following = block + 1 + AHEAD
+                if isinstance(block, int):
+                    if following < blocks:
+                        start(following)
+                else:
+                    pl.when(following < blocks)(functools.partial(start, following))
+                make_target(block + 1)
+            multiply(block, second, range(middle, depth), block + 1, block, first)
+            multiply(block + 1, first, range(depth), block + 1, block, second)
+            multiply(block + 1, second, range(middle), None, block + 1, first)
 
         squares_ref[...] = jnp.zeros_like(squares_ref)
-        push(0, 0, 0)
-        half(0, first, 0, None, ())
-        block_step(0)
-
-        @pl.loop(1, blocks - 1)
+        push(0, 0)
+        multiply(0, first, range(depth), 0, 0, ())
+        multiply(0, second, range(middle), None, 0, first)
+        for block in range(heads):
+            block_step(block)
+
+        @pl.loop(heads, blocks - 1)
         def _(block):
             block_step(block)
 
-        half(blocks - 1, second, None, blocks - 1, first)
-        for s in second:
-            take(blocks - 1, s)
-
-        for s in range(samples):
-            row = prior_ref[s : s + 1, :] - 0.5 * jnp.sum(
-                squares_ref[s].T, axis=0, keepdims=True
-            )
-            out_ref[:, s, :] = jnp.broadcast_to(row, (out_ref.shape[0], images))
+        last = blocks - 1
+        done = middle * len(first) // depth
+        left = first[done:]
+        for index, s in enumerate(second):
+            for k in range(middle, depth):
+                for q in range(2):
+                    pltpu.matmul_acc_lhs(acc[q][s], lhs(s, k), load_staged_rhs=k % 2)
+                if k + 1 < depth:
+                    push(last, k + 1)
+                elif s != second[-1]:
+                    push(last, middle)
+            if index < len(left):
+                take(last, left[index])
+            if index > 0:
+                take(last, second[index - 1])
+        for s in first[:done]:
+            finish_row(s, squares_ref[s])
+        take(last, second[-1])
+        out_ref[...] = jnp.broadcast_to(row_ref[...][None], out_ref.shape)
 
     pl.run_scoped(
         body,
@@ -288,6 +361,7 @@
     hidden_units, pixels = w_out.shape
     width = 2 * TILE
     blocks = pixels // width
+    heads = min(2, blocks - 1)
 
     def from_neighbour(value, shift):
         return lax.ppermute(
@@ -303,14 +377,15 @@
     prepared = pl.pallas_call(
         functools.partial(prepare_kernel, "tp", tp_size),
         in_specs=[hbm] * 9,
-        out_specs=[vmem] * 6,
+        out_specs=[vmem] * 7,
         out_shape=[
             jax.ShapeDtypeStruct((rows, TILE), bf16),
             jax.ShapeDtypeStruct((rows, units), bf16),
             jax.ShapeDtypeStruct((sample_count, image_count), f32),
-            jax.ShapeDtypeStruct((blocks, image_count, width), f32),
+            jax.ShapeDtypeStruct((heads, image_count, width), f32),
             jax.ShapeDtypeStruct((8, pixels), f32),
-            jax.ShapeDtypeStruct((1, hidden_units, width), bf16),
+            jax.ShapeDtypeStruct(b_out.shape, f32),
+            jax.ShapeDtypeStruct((heads, hidden_units, width), bf16),
         ],
         scratch_shapes=[
             pltpu.VMEM((sample_count, image_count, latent_dims), f32),
@@ -318,11 +393,10 @@
             pltpu.VMEM(enc_logscale.shape, f32),
             pltpu.VMEM(w_in.shape, bf16),
             pltpu.VMEM(b_in.shape, bf16),
-            pltpu.VMEM(b_out.shape, f32),
             pltpu.VMEM(pixel_logscale.shape, f32),
-            pltpu.VMEM(images.shape, bf16),
+            pltpu.VMEM((image_count, heads * width), bf16),
             pltpu.SemaphoreType.DMA((sample_count + 7,)),
-            pltpu.SemaphoreType.DMA((tp_size,)),
+            pltpu.SemaphoreType.DMA((heads, tp_size)),
         ],
         compiler_params=pltpu.CompilerParams(vmem_limit_bytes=14 << 20),
         cost_estimate=pl.CostEstimate(
@@ -334,15 +408,19 @@
     )(*map(in_hbm, (noise, enc_mean, enc_logscale, w_in, b_in, b_out, pixel_logscale, images, w_out)))
     partial = pl.pallas_call(
         functools.partial(decoder_kernel, "tp", tp_size),
-        in_specs=[vmem] * (6 + 2 * (tp_size - 1)) + [hbm],
+        in_specs=[vmem] * (7 + 2 * (tp_size - 1)) + [hbm] * 2,
         out_specs=vmem,
         out_shape=jax.ShapeDtypeStruct((devices, sample_count, image_count), f32),
         scratch_shapes=[
             pltpu.VMEM((rows, hidden_units - units), bf16),
-            pltpu.VMEM((blocks - 1, hidden_units, width), bf16),
+            pltpu.VMEM((blocks - heads, hidden_units, width), bf16),
+            pltpu.VMEM((blocks - heads, image_count, width), bf16),
+            pltpu.VMEM((blocks - heads, image_count, width), f32),
             pltpu.VMEM((sample_count, image_count, LANES), f32),
+            pltpu.VMEM((sample_count, image_count), f32),
             pltpu.VMEM((TILE, units), bf16),
-            pltpu.SemaphoreType.DMA((blocks - 1, tp_size)),
+            pltpu.SemaphoreType.DMA((blocks - heads, tp_size)),
+            pltpu.SemaphoreType.DMA((blocks - heads,)),
         ],
         compiler_params=pltpu.CompilerParams(vmem_limit_bytes=32 << 20),
         cost_estimate=pl.CostEstimate(
@@ -351,7 +429,7 @@
             transcendentals=0,
         ),
         name="decoder",
-    )(*prepared, *w_in_others, *b_in_others, in_hbm(w_out))
+    )(*prepared, *w_in_others, *b_in_others, in_hbm(images), in_hbm(w_out))
     received = lax.all_to_all(partial, ("samp", "tp"), 0, 0)
     bound, weights = pl.pallas_call(
         functools.partial(finish_kernel, "samp", tp_size, pixels * tp_size),

time: 35.3 us -> 33.6 us (0.952)
  Pallas kernels: 18.6 us -> 16.9 us
    pallas_call x1, Pallas kernels: 15.7 us -> 14.1 us  [on_device(): pl.pallas_call(functools.partial(decoder_kernel, 'tp', tp_size), in_specs...]
where the time goes in v3:
time: 33.6 us; the launch traced here: 33.5 us
  Pallas kernels  16.9 us (50%)
  blocking collectives  15.3 us (46%)
  between operations  0.67 us (2%)
  starting transfers between devices  0.64 us (2%)
    all_to_all x1, blocking collectives, on_device(): received = lax.all_to_all(partial, ('samp', 'tp'), 0, 0)  15.3 us
    pallas_call x1, Pallas kernels, on_device(): pl.pallas_call(functools.partial(decoder_kernel, 'tp', tp_size), in_specs...  14.1 us
    pallas_call x1, Pallas kernels, on_device(): pl.pallas_call(functools.partial(prepare_kernel, 'tp', tp_size), in_specs...  2.14 us
  transfers between devices with their start and end apart: 2, of which 0 were waited for; matrix products, arithmetic and copies ran while one was open for 0% of the time, Pallas kernels for 6%

profile of v3, /device:TPU:0, one launch (start us, length us, event | category | flops | bytes accessed | tf_op | source)
XLA Modules:
  0.0 33.5 jit_solution(16655509760754107663)
XLA Ops:
  0.6 0.6 %collective-permute-start = (bf16[128,512]{1,0:T(8,128)(2,1)}, bf16[128,512]{1,0:T(8,128)(2,1)S(1)}, u32[]{:S(2)}, u32[]{:S(2)}) collective-permute-start(bf16[128,512]{1,0:T(8,128)(2,1)} %w_in_hbm.1), channel_id=1, source_target_pairs={{0,1},{1,0},{2,3},{3,2},{4,5},{5,4},{6,7},{7,6},{8,9},{9,8},{10,11... | collective-permute-start | bytes 393224 | tf_op jit(solution)/shard_map/ppermute | solution.py:367
  1.2 0.1 collective-permute-start.1
  1.3 2.1 %prepare.1 = (bf16[1024,256]{1,0:T(8,128)(2,1)S(1)}, bf16[1024,512]{1,0:T(8,128)(2,1)S(1)}, f32[8,128]{1,0:T(8,128)S(1)}, f32[2,128,512]{2,1,0:T(8,128)S(1)}, f3...) custom-call(f32[128,8,128]{2,1,0:T(8,128)} %noise_hbm.1, f32[128,128]{1,0:T(8,128)} %mean_hbm.1, ...), custom_call_target="tpu_custom_call" | custom-call | flops 149946368 | bytes 2097152 | tf_op jit(solution)/shard_map/prepare/pallas_call | solution.py:377
  3.4 0.0 collective-permute-done.1.refs_1_
  3.4 0.0 collective-permute-done.refs_0_
  3.4 14.1 %decoder.1 = f32[32,8,128]{2,1,0:T(8,128)S(1)} custom-call(bf16[1024,256]{1,0:T(8,128)(2,1)S(1)} %get-tuple-element.11.latent_ref, bf16[1024,512]{1,0:T(8,128)(2,1)S(1)} %get-tuple-element.12.own_ref, f32[8,128]{1,0:T(8,128)S(1)} %get-tuple-element.13.prior_ref, f32[2,128,512]{2,1,0:T(8,128)S(1)} %get-tuple-element.14.head_target_ref, ...), custom_call_target="tpu_custom_call" | custom-call | flops 12884901888 | bytes 12582912 | tf_op jit(solution)/shard_map/decoder/pallas_call | solution.py:409
  17.6 15.3 %all_to_all.5.received_ref = f32[32,8,128]{2,1,0:T(8,128)S(1)} all-to-all(f32[32,8,128]{2,1,0:T(8,128)S(1)} %decoder.1), channel_id=1, replica_groups=mesh['samp'=16,'tp'=2] {'samp','tp'}, dimensions={0} | all-to-all | bytes 262144 | tf_op jit(solution)/shard_map/all_to_all | solution.py:433
  32.8 0.6 %finish.1 = (f32[1,128]{1,0:T(1,128)}, f32[8,128]{1,0:T(8,128)}) custom-call(f32[32,8,128]{2,1,0:T(8,128)S(1)} %all_to_all.5.received_ref), custom_call_target="tpu_custom_call" | custom-call | tf_op jit(solution)/shard_map/finish/pallas_call | solution.py:434
Async XLA Ops:
  0.6 2.8 %collective-permute-start = (bf16[128,512]{1,0:T(8,128)(2,1)}, bf16[128,512]{1,0:T(8,128)(2,1)S(1)}, u32[]{:S(2)}, u32[]{:S(2)}) collective-permute-start(bf16[128,512]{1,0:T(8,128)(2,1)} %w_in_hbm.1), channel_id=1, source_target_pairs={{0,1},{1,0},{2,3},{3,2},{4,5},{5,4},{6,7},{7,6},{8,9},{9,8},{10,11... | collective-permute-start | bytes 393224 | tf_op jit(solution)/shard_map/ppermute | solution.py:367
  1.2 2.2 %collective-permute-start.1 = (bf16[1,512]{1,0:T(2,128)(2,1)}, bf16[1,512]{1,0:T(2,128)(2,1)S(1)}, u32[]{:S(2)}, u32[]{:S(2)}) collective-permute-start(bf16[1,512]{1,0:T(2,128)(2,1)} %b_in_hbm.1), channel_id=1, source_target_pairs={{0,1},{1,0},{2,3},{3,2},{4,5},{5,4},{6,7},{7,6},{8,9},{9,8},{10,11... | collective-permute-start | bytes 3080 | tf_op jit(solution)/shard_map/ppermute | solution.py:367

commit v4 on v3

--- a/solution.py
+++ b/solution.py
@@ -43,12 +43,10 @@
     b_in_hbm,
     bias_hbm,
     pixel_logscale_hbm,
-    image_hbm,
     w_hbm,
     latent_ref,
     hidden_ref,
     prior_ref,
-    target_ref,
     inverse_ref,
     bias_ref,
     head_ref,
@@ -58,12 +56,11 @@
     w_in_ref,
     b_in_ref,
     pixel_logscale_ref,
-    image_ref,
     sem,
     head_sem,
 ):
     samples, images, latent_dims = noise_ref.shape
-    heads, _, width = target_ref.shape
+    heads, _, width = head_ref.shape
     pairs = [(noise_hbm.at[:, s, :], noise_ref.at[s]) for s in range(samples)] + [
         (mean_hbm, mean_ref),
         (logscale_hbm, logscale_ref),
@@ -71,7 +68,6 @@
         (b_in_hbm, b_in_ref),
         (pixel_logscale_hbm, pixel_logscale_ref),
         (bias_hbm, bias_ref),
-        (image_hbm.at[:, pl.ds(0, heads * width)], image_ref),
     ]
     copies = [pltpu.make_async_copy(a, b, sem.at[i]) for i, (a, b) in enumerate(pairs)]
     head = []
@@ -112,11 +108,6 @@
     )
     for copy in copies[samples + 5 :]:
         copy.wait()
-    for block in range(heads):
-        columns = slice(block * width, (block + 1) * width)
-        target_ref[block] = (
-            image_ref[:, columns].astype(jnp.float32) - bias_ref[:, columns]
-        ) * inverse_ref[:1, columns]
     for copy in head:
         copy.wait()
 
@@ -127,7 +118,6 @@
     latent_ref,
     own_ref,
     prior_ref,
-    head_target_ref,
     inverse_ref,
     bias_ref,
     head_ref,
@@ -135,21 +125,19 @@
 ):
     w_in_refs, b_in_refs = refs[: tp_size - 1], refs[tp_size - 1 : 2 * tp_size - 2]
     (
-        image_hbm,
+        image_ref,
         w_hbm,
         out_ref,
         hidden_ref,
         w_ref,
-        image_ref,
         target_ref,
         squares_ref,
         row_ref,
         w_in_pad_ref,
         sem,
-        image_sem,
     ) = refs[2 * tp_size - 2 :]
-    heads, images, width = head_target_ref.shape
-    blocks = heads + w_ref.shape[0]
+    heads, _, width = head_ref.shape
+    blocks, images, _ = target_ref.shape
     samples = squares_ref.shape[0]
     units = own_ref.shape[1]
     latent_dims = w_in_refs[0].shape[0]
@@ -157,12 +145,7 @@
 
     def fetches(block):
         at = block - heads
-        image = pltpu.make_async_copy(
-            image_hbm.at[:, pl.ds(pl.multiple_of(block * width, width), width)],
-            image_ref.at[at], image_sem.at[at]
-        )
-        w_copies = w_block(w_hbm, w_ref.at[at], sem.at[at], tp_axis, tp_size, block)
-        return w_copies + [image]
+        return w_block(w_hbm, w_ref.at[at], sem.at[at], tp_axis, tp_size, block)
 
     def start(block):
         for copy in fetches(block):
@@ -228,8 +211,8 @@
 
         def make_target(block):
             columns = columns_of(block, 0, width)
-            image = image_ref[block - heads].astype(jnp.float32)
-            target_ref[block - heads] = (image - bias_ref[:, columns]) * inverse_ref[:1, columns]
+            image = image_ref[:, columns].astype(jnp.float32)
+            target_ref[block] = (image - bias_ref[:, columns]) * inverse_ref[:1, columns]
 
         def finish_row(s, total):
             lanes = jnp.sum(total.T, axis=0, keepdims=True)
@@ -241,10 +224,7 @@
                 product = pltpu.matmul_pop(acc[q][s]).reshape(images // 8, 8, TILE)
                 inverse = inverse_ref[:, columns_of(block, q * TILE, TILE)]
                 wide = slice(q * TILE, (q + 1) * TILE)
-                if in_head(block):
-                    target = head_target_ref[block, :, wide]
-                else:
-                    target = target_ref[block - heads, :, wide]
+                target = target_ref[block, :, wide]
                 scaled = target.reshape(images // 8, 8, TILE) - product * inverse[None]
                 square = (scaled * scaled).reshape(images, TILE)
                 for lane in range(0, TILE, LANES):
@@ -283,13 +263,14 @@
                         start(following)
                 else:
                     pl.when(following < blocks)(functools.partial(start, following))
-                make_target(block + 1)
+            make_target(block + 1)
             multiply(block, second, range(middle, depth), block + 1, block, first)
             multiply(block + 1, first, range(depth), block + 1, block, second)
             multiply(block + 1, second, range(middle), None, block + 1, first)
 
         squares_ref[...] = jnp.zeros_like(squares_ref)
         push(0, 0)
+        make_target(0)
         multiply(0, first, range(depth), 0, 0, ())
         multiply(0, second, range(middle), None, 0, first)
         for block in range(heads):
@@ -376,13 +357,12 @@
     in_hbm = lambda value: pltpu.with_memory_space_constraint(value, pltpu.HBM)
     prepared = pl.pallas_call(
         functools.partial(prepare_kernel, "tp", tp_size),
-        in_specs=[hbm] * 9,
-        out_specs=[vmem] * 7,
+        in_specs=[hbm] * 8,
+        out_specs=[vmem] * 6,
         out_shape=[
             jax.ShapeDtypeStruct((rows, TILE), bf16),
             jax.ShapeDtypeStruct((rows, units), bf16),
             jax.ShapeDtypeStruct((sample_count, image_count), f32),
-            jax.ShapeDtypeStruct((heads, image_count, width), f32),
             jax.ShapeDtypeStruct((8, pixels), f32),
             jax.ShapeDtypeStruct(b_out.shape, f32),
             jax.ShapeDtypeStruct((heads, hidden_units, width), bf16),
@@ -394,8 +374,7 @@
             pltpu.VMEM(w_in.shape, bf16),
             pltpu.VMEM(b_in.shape, bf16),
             pltpu.VMEM(pixel_logscale.shape, f32),
-            pltpu.VMEM((image_count, heads * width), bf16),
-            pltpu.SemaphoreType.DMA((sample_count + 7,)),
+            pltpu.SemaphoreType.DMA((sample_count + 6,)),
             pltpu.SemaphoreType.DMA((heads, tp_size)),
         ],
         compiler_params=pltpu.CompilerParams(vmem_limit_bytes=14 << 20),
@@ -405,22 +384,20 @@
             transcendentals=pixels,
         ),
         name="prepare",
-    )(*map(in_hbm, (noise, enc_mean, enc_logscale, w_in, b_in, b_out, pixel_logscale, images, w_out)))
+    )(*map(in_hbm, (noise, enc_mean, enc_logscale, w_in, b_in, b_out, pixel_logscale, w_out)))
     partial = pl.pallas_call(
         functools.partial(decoder_kernel, "tp", tp_size),
-        in_specs=[vmem] * (7 + 2 * (tp_size - 1)) + [hbm] * 2,
+        in_specs=[vmem] * (7 + 2 * (tp_size - 1)) + [hbm],
         out_specs=vmem,
         out_shape=jax.ShapeDtypeStruct((devices, sample_count, image_count), f32),
         scratch_shapes=[
             pltpu.VMEM((rows, hidden_units - units), bf16),
             pltpu.VMEM((blocks - heads, hidden_units, width), bf16),
-            pltpu.VMEM((blocks - heads, image_count, width), bf16),
-            pltpu.VMEM((blocks - heads, image_count, width), f32),
+            pltpu.VMEM((blocks, image_count, width), f32),
             pltpu.VMEM((sample_count, image_count, LANES), f32),
             pltpu.VMEM((sample_count, image_count), f32),
             pltpu.VMEM((TILE, units), bf16),
             pltpu.SemaphoreType.DMA((blocks - heads, tp_size)),
-            pltpu.SemaphoreType.DMA((blocks - heads,)),
         ],
         compiler_params=pltpu.CompilerParams(vmem_limit_bytes=32 << 20),
         cost_estimate=pl.CostEstimate(
@@ -429,7 +406,7 @@
             transcendentals=0,
         ),
         name="decoder",
-    )(*prepared, *w_in_others, *b_in_others, in_hbm(images), in_hbm(w_out))
+    )(*prepared, *w_in_others, *b_in_others, images, in_hbm(w_out))
     received = lax.all_to_all(partial, ("samp", "tp"), 0, 0)
     bound, weights = pl.pallas_call(
         functools.partial(finish_kernel, "samp", tp_size, pixels * tp_size),

time: 33.6 us -> 33.4 us (level)
  no operation moved by 1% of the time
where the time goes in v4:
time: 33.4 us; the launch traced here: 33.2 us
  Pallas kernels  16.6 us (50%)
  blocking collectives  15.3 us (46%)
  between operations  0.68 us (2%)
  starting transfers between devices  0.64 us (2%)
    all_to_all x1, blocking collectives, on_device(): received = lax.all_to_all(partial, ('samp', 'tp'), 0, 0)  15.3 us
    pallas_call x1, Pallas kernels, on_device(): pl.pallas_call(functools.partial(decoder_kernel, 'tp', tp_size), in_specs...  13.9 us
    pallas_call x1, Pallas kernels, on_device(): pl.pallas_call(functools.partial(prepare_kernel, 'tp', tp_size), in_specs...  2.05 us
  transfers between devices with their start and end apart: 2, of which 0 were waited for; matrix products, arithmetic and copies ran while one was open for 0% of the time, Pallas kernels for 6%

profile of v4, /device:TPU:0, one launch (start us, length us, event | category | flops | bytes accessed | tf_op | source)
XLA Modules:
  0.0 33.2 jit_solution(5814649075734877276)
XLA Ops:
  0.6 0.0 copy-start
  0.6 0.6 %collective-permute-start = (bf16[128,512]{1,0:T(8,128)(2,1)}, bf16[128,512]{1,0:T(8,128)(2,1)S(1)}, u32[]{:S(2)}, u32[]{:S(2)}) collective-permute-start(bf16[128,512]{1,0:T(8,128)(2,1)} %w_in_hbm.1), channel_id=1, source_target_pairs={{0,1},{1,0},{2,3},{3,2},{4,5},{5,4},{6,7},{7,6},{8,9},{9,8},{10,11... | collective-permute-start | bytes 393224 | tf_op jit(solution)/shard_map/ppermute | solution.py:348
  1.2 0.1 collective-permute-start.1
  1.3 2.1 %prepare.1 = (bf16[1024,256]{1,0:T(8,128)(2,1)S(1)}, bf16[1024,512]{1,0:T(8,128)(2,1)S(1)}, f32[8,128]{1,0:T(8,128)S(1)}, f32[8,6144]{1,0:T(8,128)S(1)}, f32[1,6...) custom-call(f32[128,8,128]{2,1,0:T(8,128)} %noise_hbm.1, f32[128,128]{1,0:T(8,128)} %mean_hbm.1, ...), custom_call_target="tpu_custom_call" | custom-call | flops 149946368 | bytes 2097152 | tf_op jit(solution)/shard_map/prepare/pallas_call | solution.py:358
  3.3 0.0 collective-permute-done.1.refs_1_
  3.3 0.0 collective-permute-done.refs_0_
  3.4 0.0 copy-done
  3.4 13.9 %decoder.1 = f32[32,8,128]{2,1,0:T(8,128)S(1)} custom-call(bf16[1024,256]{1,0:T(8,128)(2,1)S(1)} %get-tuple-element.10.latent_ref, bf16[1024,512]{1,0:T(8,128)(2,1)S(1)} %get-tuple-element.11.own_ref, f32[8,128]{1,0:T(8,128)S(1)} %get-tuple-element.12.prior_ref, f32[8,6144]{1,0:T(8,128)S(1)} %get-tuple-element.13.inverse_ref, ...), custom_call_target="tpu_custom_call" | custom-call | flops 12884901888 | bytes 12582912 | tf_op jit(solution)/shard_map/decoder/pallas_call | solution.py:388
  17.3 15.3 %all_to_all.5.received_ref = f32[32,8,128]{2,1,0:T(8,128)S(1)} all-to-all(f32[32,8,128]{2,1,0:T(8,128)S(1)} %decoder.1), channel_id=1, replica_groups=mesh['samp'=16,'tp'=2] {'samp','tp'}, dimensions={0} | all-to-all | bytes 262144 | tf_op jit(solution)/shard_map/all_to_all | solution.py:410
  32.6 0.6 %finish.1 = (f32[1,128]{1,0:T(1,128)}, f32[8,128]{1,0:T(8,128)}) custom-call(f32[32,8,128]{2,1,0:T(8,128)S(1)} %all_to_all.5.received_ref), custom_call_target="tpu_custom_call" | custom-call | tf_op jit(solution)/shard_map/finish/pallas_call | solution.py:411
Async XLA Ops:
  0.6 2.7 %copy-start = (bf16[128,6144]{1,0:T(8,128)(2,1)S(1)}, bf16[128,6144]{1,0:T(8,128)(2,1)}, u32[]{:S(2)}) copy-start(bf16[128,6144]{1,0:T(8,128)(2,1)} %refs_2_.1) | copy-start | bytes 4718596
  0.6 2.7 %collective-permute-start = (bf16[128,512]{1,0:T(8,128)(2,1)}, bf16[128,512]{1,0:T(8,128)(2,1)S(1)}, u32[]{:S(2)}, u32[]{:S(2)}) collective-permute-start(bf16[128,512]{1,0:T(8,128)(2,1)} %w_in_hbm.1), channel_id=1, source_target_pairs={{0,1},{1,0},{2,3},{3,2},{4,5},{5,4},{6,7},{7,6},{8,9},{9,8},{10,11... | collective-permute-start | bytes 393224 | tf_op jit(solution)/shard_map/ppermute | solution.py:348
  1.2 2.1 %collective-permute-start.1 = (bf16[1,512]{1,0:T(2,128)(2,1)}, bf16[1,512]{1,0:T(2,128)(2,1)S(1)}, u32[]{:S(2)}, u32[]{:S(2)}) collective-permute-start(bf16[1,512]{1,0:T(2,128)(2,1)} %b_in_hbm.1), channel_id=1, source_target_pairs={{0,1},{1,0},{2,3},{3,2},{4,5},{5,4},{6,7},{7,6},{8,9},{9,8},{10,11... | collective-permute-start | bytes 3080 | tf_op jit(solution)/shard_map/ppermute | solution.py:348

commit v5 on v4

--- a/solution.py
+++ b/solution.py
@@ -41,14 +41,12 @@
     logscale_hbm,
     w_in_hbm,
     b_in_hbm,
-    bias_hbm,
     pixel_logscale_hbm,
     w_hbm,
     latent_ref,
     hidden_ref,
     prior_ref,
     inverse_ref,
-    bias_ref,
     head_ref,
     noise_ref,
     mean_ref,
@@ -67,7 +65,6 @@
         (w_in_hbm, w_in_ref),
         (b_in_hbm, b_in_ref),
         (pixel_logscale_hbm, pixel_logscale_ref),
-        (bias_hbm, bias_ref),
     ]
     copies = [pltpu.make_async_copy(a, b, sem.at[i]) for i, (a, b) in enumerate(pairs)]
     head = []
@@ -106,8 +103,6 @@
     inverse_ref[...] = jnp.broadcast_to(
         jnp.exp(-pixel_logscale_ref[...]), inverse_ref.shape
     )
-    for copy in copies[samples + 5 :]:
-        copy.wait()
     for copy in head:
         copy.wait()
 
@@ -357,14 +352,13 @@
     in_hbm = lambda value: pltpu.with_memory_space_constraint(value, pltpu.HBM)
     prepared = pl.pallas_call(
         functools.partial(prepare_kernel, "tp", tp_size),
-        in_specs=[hbm] * 8,
-        out_specs=[vmem] * 6,
+        in_specs=[hbm] * 7,
+        out_specs=[vmem] * 5,
         out_shape=[
             jax.ShapeDtypeStruct((rows, TILE), bf16),
             jax.ShapeDtypeStruct((rows, units), bf16),
             jax.ShapeDtypeStruct((sample_count, image_count), f32),
             jax.ShapeDtypeStruct((8, pixels), f32),
-            jax.ShapeDtypeStruct(b_out.shape, f32),
             jax.ShapeDtypeStruct((heads, hidden_units, width), bf16),
         ],
         scratch_shapes=[
@@ -374,7 +368,7 @@
             pltpu.VMEM(w_in.shape, bf16),
             pltpu.VMEM(b_in.shape, bf16),
             pltpu.VMEM(pixel_logscale.shape, f32),
-            pltpu.SemaphoreType.DMA((sample_count + 6,)),
+            pltpu.SemaphoreType.DMA((sample_count + 5,)),
             pltpu.SemaphoreType.DMA((heads, tp_size)),
         ],
         compiler_params=pltpu.CompilerParams(vmem_limit_bytes=14 << 20),
@@ -384,7 +378,7 @@
             transcendentals=pixels,
         ),
         name="prepare",
-    )(*map(in_hbm, (noise, enc_mean, enc_logscale, w_in, b_in, b_out, pixel_logscale, w_out)))
+    )(*map(in_hbm, (noise, enc_mean, enc_logscale, w_in, b_in, pixel_logscale, w_out)))
     partial = pl.pallas_call(
         functools.partial(decoder_kernel, "tp", tp_size),
         in_specs=[vmem] * (7 + 2 * (tp_size - 1)) + [hbm],
@@ -406,7 +400,7 @@
             transcendentals=0,
         ),
         name="decoder",
-    )(*prepared, *w_in_others, *b_in_others, images, in_hbm(w_out))
+    )(*prepared[:4], b_out, prepared[4], *w_in_others, *b_in_others, images, in_hbm(w_out))
     received = lax.all_to_all(partial, ("samp", "tp"), 0, 0)
     bound, weights = pl.pallas_call(
         functools.partial(finish_kernel, "samp", tp_size, pixels * tp_size),

time: 33.4 us -> 33.7 us (level)
  transfers between devices with their start and end apart: 2 -> 2, of which waited for: 0 -> 0; matrix products, arithmetic and copies ran while one was open for 0% -> 0% of each run, Pallas kernels for 6% -> 7%
where the time goes in v5:
time: 33.7 us; the launch traced here: 33.5 us
  Pallas kernels  16.9 us (50%)
  blocking collectives  15.3 us (45%)
  between operations  0.7 us (2%)
  starting transfers between devices  0.64 us (2%)
    all_to_all x1, blocking collectives, on_device(): received = lax.all_to_all(partial, ('samp', 'tp'), 0, 0)  15.3 us
    pallas_call x1, Pallas kernels, on_device(): pl.pallas_call(functools.partial(decoder_kernel, 'tp', tp_size), in_specs...  13.9 us
    pallas_call x1, Pallas kernels, on_device(): pl.pallas_call(functools.partial(prepare_kernel, 'tp', tp_size), in_specs...  2.28 us
  transfers between devices with their start and end apart: 2, of which 0 were waited for; matrix products, arithmetic and copies ran while one was open for 0% of the time, Pallas kernels for 7%

profile of v5, /device:TPU:0, one launch (start us, length us, event | category | flops | bytes accessed | tf_op | source)
XLA Modules:
  0.0 33.5 jit_solution(1836472111112889744)
XLA Ops:
  0.6 0.0 copy-start.1
  0.6 0.0 copy-start
  0.7 0.6 %collective-permute-start = (bf16[128,512]{1,0:T(8,128)(2,1)}, bf16[128,512]{1,0:T(8,128)(2,1)S(1)}, u32[]{:S(2)}, u32[]{:S(2)}) collective-permute-start(bf16[128,512]{1,0:T(8,128)(2,1)} %w_in_hbm.1), channel_id=1, source_target_pairs={{0,1},{1,0},{2,3},{3,2},{4,5},{5,4},{6,7},{7,6},{8,9},{9,8},{10,11... | collective-permute-start | bytes 393224 | tf_op jit(solution)/shard_map/ppermute | solution.py:343
  1.2 0.1 collective-permute-start.1
  1.3 2.3 %prepare.1 = (bf16[1024,256]{1,0:T(8,128)(2,1)S(1)}, bf16[1024,512]{1,0:T(8,128)(2,1)S(1)}, f32[8,128]{1,0:T(8,128)S(1)}, f32[8,6144]{1,0:T(8,128)S(1)}, bf16[2,1024,512]{2,1,0:T(8,128)(2,1)S(1)}) custom-call(f32[128,8,128]{2,1,0:T(8,128)} %noise_hbm.1, f32[128,128]{1,0:T(8,128)} %mean_hbm.1, f32[128,128]{1,0:T(8,128)} %logscale_hbm.1, ...), custom_call_target="tpu_custom_call" | custom-call | flops 149946368 | bytes 2097152 | tf_op jit(solution)/shard_map/prepare/pallas_call | solution.py:353
  3.6 0.0 collective-permute-done.1.refs_1_
  3.6 0.0 collective-permute-done.refs_0_
  3.6 0.0 copy-done.1
  3.6 0.0 copy-done
  3.6 13.9 %decoder.1 = f32[32,8,128]{2,1,0:T(8,128)S(1)} custom-call(bf16[1024,256]{1,0:T(8,128)(2,1)S(1)} %get-tuple-element.9.latent_ref, bf16[1024,512]{1,0:T(8,128)(2,1)S(1)} %get-tuple-element.10.own_ref, f32[8,128]{1,0:T(8,128)S(1)} %get-tuple-element.11.prior_ref, f32[8,6144]{1,0:T(8,128)S(1)} %get-tuple-element.12.inverse_ref, f32[1,6144]{1,0:T(1,128)S(1)} %copy-done.1, ...), custom_call_target="tpu_custom_call" | custom-call | flops 12884901888 | bytes 12582912 | tf_op jit(solution)/shard_map/decoder/pallas_call | solution.py:382
  17.6 15.3 %all_to_all.5.received_ref = f32[32,8,128]{2,1,0:T(8,128)S(1)} all-to-all(f32[32,8,128]{2,1,0:T(8,128)S(1)} %decoder.1), channel_id=1, replica_groups=mesh['samp'=16,'tp'=2] {'samp','tp'}, dimensions={0} | all-to-all | bytes 262144 | tf_op jit(solution)/shard_map/all_to_all | solution.py:404
  32.8 0.6 %finish.1 = (f32[1,128]{1,0:T(1,128)}, f32[8,128]{1,0:T(8,128)}) custom-call(f32[32,8,128]{2,1,0:T(8,128)S(1)} %all_to_all.5.received_ref), custom_call_target="tpu_custom_call" | custom-call | tf_op jit(solution)/shard_map/finish/pallas_call | solution.py:405
Async XLA Ops:
  0.6 3.0 %copy-start.1 = (f32[1,6144]{1,0:T(1,128)S(1)}, f32[1,6144]{1,0:T(1,128)}, u32[]{:S(2)}) copy-start(f32[1,6144]{1,0:T(1,128)} %bias_ref.1) | copy-start | bytes 73732
  0.6 3.0 %copy-start = (bf16[128,6144]{1,0:T(8,128)(2,1)S(1)}, bf16[128,6144]{1,0:T(8,128)(2,1)}, u32[]{:S(2)}) copy-start(bf16[128,6144]{1,0:T(8,128)(2,1)} %refs_2_.1) | copy-start | bytes 4718596
  0.7 2.9 %collective-permute-start = (bf16[128,512]{1,0:T(8,128)(2,1)}, bf16[128,512]{1,0:T(8,128)(2,1)S(1)}, u32[]{:S(2)}, u32[]{:S(2)}) collective-permute-start(bf16[128,512]{1,0:T(8,128)(2,1)} %w_in_hbm.1), channel_id=1, source_target_pairs={{0,1},{1,0},{2,3},{3,2},{4,5},{5,4},{6,7},{7,6},{8,9},{9,8},{10,11... | collective-permute-start | bytes 393224 | tf_op jit(solution)/shard_map/ppermute | solution.py:343
  1.2 2.4 %collective-permute-start.1 = (bf16[1,512]{1,0:T(2,128)(2,1)}, bf16[1,512]{1,0:T(2,128)(2,1)S(1)}, u32[]{:S(2)}, u32[]{:S(2)}) collective-permute-start(bf16[1,512]{1,0:T(2,128)(2,1)} %b_in_hbm.1), channel_id=1, source_target_pairs={{0,1},{1,0},{2,3},{3,2},{4,5},{5,4},{6,7},{7,6},{8,9},{9,8},{10,11... | collective-permute-start | bytes 3080 | tf_op jit(solution)/shard_map/ppermute | solution.py:343
